TPU v7x, 128 devices: a whole 4x4x4 slice. The times are simulated.
128 devices in a mesh: dp: 8 (over x, core), tensor: 16 (over y, z).
Axes of the slice: x: 4, y: 4, z: 4, core: 2. Of those that a mesh axis runs over, the one named last changes fastest.
Arguments:
- hidden: bfloat16 [16, 64, 4608], P('dp', 'tensor'), may hold values from -6 to 6
- gain: float32 [4608], replicated, may hold values from 0.5 to 1.5
- labels: int32 [16, 64], P('dp', 'tensor'), may hold values from 0 to 255999
- lengths: int32 [16], replicated, may hold values from 1 to 64
- embed: bfloat16 [256000, 4608], P(('dp', 'tensor')), may hold values from -0.375 to 0.375
Outputs:
- token_logprob: float32 [16, 64], P('dp', 'tensor')
- mean_nll: float32 [], replicated
- z_loss: float32 [], replicated
All inputs are finite; a program needn't handle non-finite values.
Results may differ from a plain program's by a relative error of at most 0.00058.
Values may be sent and summed in bfloat16 or wider, within the bound.
No kernel may reach another device: no remote copies, remote signals or barrier semaphores. Data moves between devices by JAX's collectives and lax.ppermute only.
A program may use at most 128 MiB of HBM per device.

v0:
```python
import jax
import jax.numpy as jnp
from jax import lax
from jax.sharding import Mesh
from jax.sharding import PartitionSpec as P

CAP = 30
TENSOR = ("tensor_0", "tensor_1")
DP = ("dp_0", "dp_1")
DP_TENSOR = ("dp_0", "dp_1", "tensor_0", "tensor_1")


def joined_along(pieces, dim):
    lengths = list(pieces.shape[1:])
    lengths[dim] *= pieces.shape[0]
    return jnp.moveaxis(pieces, 0, dim).reshape(lengths)


def gather_in_order(value, axes, order):
    pieces = value[None]
    for k in order:
        pieces = lax.all_gather(pieces, axes[k], axis=0, tiled=True)
    block = [lax.axis_size(axes[k]) for k in reversed(order)]
    pieces = pieces.reshape(*block, *value.shape)
    turned = sorted(range(len(order)), key=lambda place: order[len(order) - 1 - place])
    return pieces.transpose(*turned, *range(len(order), pieces.ndim)).reshape(-1, *value.shape)


def gathered_by_axis(value, axes, order, dim):
    return joined_along(gather_in_order(value, axes, order), dim)


def one_axis_at_a_time(value, axes):
    for axis in axes:
        value = lax.psum(value, axis)
    return value


def normalize(rows, gain):
    values = rows.astype(jnp.float32)
    meansq = jnp.mean(values * values, axis=-1, keepdims=True)
    return (values * lax.rsqrt(meansq + 1e-06) * gain).astype(jnp.bfloat16)


def per_device(hidden, gain, labels, lengths, embed):
    n_tensor = lax.axis_size(TENSOR)
    n_all = lax.axis_size(DP) * n_tensor
    seqs, stretch, width = hidden.shape
    vocab_dev = embed.shape[0]
    rows_local = seqs * stretch
    total_rows = rows_local * n_all
    flat = hidden.reshape(rows_local, width)
    row_ids = jnp.arange(total_rows)
    owner = row_ids // rows_local
    within = row_ids % rows_local
    batch_ids = owner // n_tensor * seqs + within // stretch
    positions = owner % n_tensor * stretch + within % stretch
    live_all = (positions < jnp.take(lengths, batch_ids)).astype(jnp.float32)
    all_labels = gathered_by_axis(labels.reshape(rows_local), DP_TENSOR, (0, 2, 3, 1), 0)
    rows = normalize(lax.all_gather(flat, DP_TENSOR, axis=0, tiled=True), gain)
    values = lax.dot_general(
        rows, embed, (((1,), (1,)), ((), ())), preferred_element_type=jnp.float32
    )
    capped = CAP * jnp.tanh(values / CAP)
    sumexp = jnp.sum(jnp.exp(capped), axis=1)
    first = lax.axis_index(DP_TENSOR) * vocab_dev
    local = all_labels - first
    inside = (local >= 0) & (local < vocab_dev)
    chosen = jnp.take_along_axis(capped, jnp.clip(local, 0, vocab_dev - 1)[:, None], axis=1)[:, 0]
    picked = jnp.where(inside, chosen, jnp.float32(0.0))
    own_start = lax.axis_index(DP_TENSOR) * rows_local
    sum_total, pick_total = (
        one_axis_at_a_time(sumexp, DP_TENSOR),
        one_axis_at_a_time(picked, DP_TENSOR),
    )
    own_sum = lax.dynamic_slice_in_dim(sum_total, own_start, rows_local)
    own_pick = lax.dynamic_slice_in_dim(pick_total, own_start, rows_local)
    own_live = lax.dynamic_slice_in_dim(live_all, own_start, rows_local)
    lse = jnp.log(own_sum)
    token = own_live * (own_pick - lse)
    nll_sum, count, square_sum = (
        one_axis_at_a_time(-jnp.sum(token), DP_TENSOR),
        one_axis_at_a_time(jnp.sum(own_live), DP_TENSOR),
        one_axis_at_a_time(jnp.sum(own_live * lse * lse), DP_TENSOR),
    )
    mean_nll = nll_sum / count
    z_loss = 0.01 * square_sum / count
    return (token.reshape(seqs, stretch), mean_nll, z_loss)


def solution(mesh):
    finer = Mesh(mesh.devices.reshape(4, 2, 4, 4), ("dp_0", "dp_1", "tensor_0", "tensor_1"))
    placed = (P(DP, TENSOR, None), P(), P(DP, TENSOR), P(), P(DP_TENSOR, None))
    return jax.shard_map(
        per_device,
        mesh=finer,
        in_specs=placed,
        out_specs=(P(DP, TENSOR), P(), P()),
        check_vma=False,
    )
```

profile of v0, /device:TPU:0, one launch (start us, length us, event | category | flops | bytes accessed | tf_op | source)
XLA Modules:
  0.0 235.7 jit_solution(905636388065802860)
XLA Ops:
  7.2 0.0 copy-start.1
  7.2 0.0 all-gather.6.cloned.1.call-start
  7.2 1.5 reshape.258
  8.8 0.0 all-gather.6.cloned.1.call-update
  8.8 0.8 reshape.330
  9.5 9.8 %all-gather = s32[4,1,8]{2,1,0:T(1,128)S(1)} all-gather(s32[1,1,8]{2,1,0:T(1,128)S(1)} %reshape.330), channel_id=1, replica_groups=mesh['dp_0'=4,'dp_1'=2,'tensor_0'=4,'tensor_1'=4] {'dp_0'}, dimensions={0}, use_global_device_ids=true | all-gather | bytes 160 | tf_op jit(solution)/shard_map/all_gather | solution.py:22
  19.4 11.3 %all-gather.1 = s32[4,4,8]{2,1,0:T(4,128)S(1)} all-gather(s32[1,4,8]{2,1,0:T(4,128)S(1)} %bitcast.36), channel_id=1, replica_groups=mesh['dp_0'=4,'dp_1'=2,'tensor_0'=4,'tensor_1'=4] {'tensor_0'}, dimensions={0}, use_global_device_ids=true | all-gather | bytes 640 | tf_op jit(solution)/shard_map/all_gather | solution.py:22
  30.7 0.1 copy.22
  30.8 13.2 %all-gather.2 = s32[4,16,8]{1,2,0:T(8,128)S(1)} all-gather(s32[1,16,8]{1,2,0:T(8,128)S(1)} %copy.22), channel_id=1, replica_groups=mesh['dp_0'=4,'dp_1'=2,'tensor_0'=4,'tensor_1'=4] {'tensor_1'}, dimensions={0}, use_global_device_ids=true | all-gather | bytes 2560 | tf_op jit(solution)/shard_map/all_gather | solution.py:22
  44.0 0.1 reshape.336
  44.1 1.8 all-gather.3
  45.9 0.1 copy.26
  46.0 0.1 min.24
  46.1 0.1 min.22
  46.2 0.1 copy.24
  46.4 0.1 and.146
  46.5 0.1 compare_reduce_fusion
  46.6 0.1 compare_reduce_fusion.1
  46.6 0.1 compare_reduce_fusion.2
  46.7 0.1 compare_reduce_fusion.3
  46.7 0.1 compare_reduce_fusion.4
  46.8 0.1 compare_reduce_fusion.5
  46.8 0.1 compare_reduce_fusion.6
  46.9 0.1 compare_reduce_fusion.7
  47.0 0.1 compare_reduce_fusion.8
  47.0 2.0 fusion.37
  49.0 4.4 %compare_select_fusion.2 = s32[1024,1]{0,1:T(1,128)S(1)} fusion(s32[]{:T(128)} %bitcast.9, s32[]{:T(128)} %bitcast.10, s32[]{:T(128)} %bitcast.11, s32[]{:T(128)} %bitcast.12, s32[]{:T(128)} %bitcast.13, s32[]{:T(128)} %bitcast.15, s32[]{:T(128)} %bitcast.14), kind=kLoop, calls=%fused_computation.22 | loop fusion | flops 60416 | bytes 4124 | tf_op jit(solution)/shard_map/jit(_take)/gather | solution.py:58
  53.5 5.8 %fusion.34 = f32[1024]{0:T(1024)S(1)} fusion(pred[1024]{0:T(1024)(128)(4,1)S(1)} %compare_reduce_fusion, pred[1024]{0:T(1024)(128)(4,1)S(1)} %compare_reduce_fusion.1, pred[1024]{0:T(1024)(128)(4,1)S(1)} %compare_reduce_fusion.2, pred[1024]{0:T(1024)(128)(4,1)S(1)} %compare_reduce_fusion.3, pred[1024]{0:T(1024)(128)(4,1)S(1)} %compare_reduce_fusion.4, ...), kind=kLoop, calls=%fused_computation.90 | loop fusion | flops 73728 | bytes 17444 | tf_op jit(solution)/shard_map/convert_element_type | solution.py:58
  59.3 24.7 %all-gather.6.cloned.1.call-done = bf16[1024,4608]{1,0:T(8,128)(2,1)} async-done(((bf16[8,4608]{1,0:T(8,128)(2,1)}), bf16[1024,4608]{1,0:T(8,128)(2,1)}) %all-gather.6.cloned.1.call-update) | async-done | bytes 9437200 | tf_op jit(solution)/shard_map/all_gather | solution.py:60
  84.0 0.0 copy-start
  84.0 5.7 %fusion = f32[1024]{0:T(1024)S(1)} fusion(bf16[1024,4608]{1,0:T(8,128)(2,1)} %all-gather.6.cloned.1.call-done), kind=kLoop, calls=%fused_computation.3 | loop fusion | flops 14154752 | bytes 9441280 | tf_op jit(solution)/shard_map/reduce_sum | solution.py:41
  89.7 0.0 copy-done.1
  89.7 0.6 copy-done
  90.3 26.1 %exponential_reduce_fusion = (f32[1024]{0:T(1024)S(1)}, f32[1024,2000]{0,1:T(8,128)}) fusion(bf16[2000,4608]{1,0:T(8,128)(2,1)} %param.9, bf16[1024,4608]{1,0:T(8,128)(2,1)S(1)} %copy-done, f32[4608]{0:T(1024)S(1)} %copy-done.1, f32[1024]{0:T(1024)S(1)} %add_rsqrt_fusion), kind=kOutput, calls=%fused_computation.9 | convolution fusion | flops 18899386368 | bytes 36087808 | tf_op jit(solution)/shard_map/dot_general | solution.py:61
  116.4 45.1 %gather_fusion = f32[1024]{0:T(1024)S(1)} fusion(f32[1024,2000]{0,1:T(8,128)} %get-tuple-element.46, s32[1024]{0:T(1024)S(1)} %bitcast.31), kind=kCustom, calls=%fused_computation | custom fusion | bytes 16384 | tf_op jit(solution)/shard_map/jit(take_along_axis)/gather | solution.py:69
  161.5 7.8 %all-reduce.5 = (f32[1024]{0:T(1024)S(1)}, f32[1024]{0:T(1024)S(1)}) all-reduce(f32[1024]{0:T(1024)S(1)} %select_select_fusion.1, f32[1024]{0:T(1024)S(1)} %get-tuple-element.45), channel_id=1, replica_groups=mesh['dp_0'=4,'dp_1'=2,'tensor_0'=4,'tensor_1'=4] {'dp_0'}, use_global_device_ids=true, to_apply=%region_1.2 | all-reduce | flops 2048 | bytes 16384 | tf_op jit(solution)/shard_map/psum | solution.py:35
  169.4 2.5 %all-reduce.7 = (f32[1024]{0:T(1024)S(1)}, f32[1024]{0:T(1024)S(1)}) all-reduce(f32[1024]{0:T(1024)S(1)} %get-tuple-element.18, f32[1024]{0:T(1024)S(1)} %get-tuple-element.19), channel_id=1, replica_groups=mesh['dp_0'=4,'dp_1'=2,'tensor_0'=4,'tensor_1'=4] {'dp_1'}, use_global_device_ids=true, to_apply=%region_2.3 | all-reduce | flops 2048 | bytes 16384 | tf_op jit(solution)/shard_map/psum | solution.py:35
  171.9 8.4 %all-reduce.3 = (f32[1024]{0:T(1024)S(1)}, f32[1024]{0:T(1024)S(1)}) all-reduce(f32[1024]{0:T(1024)S(1)} %get-tuple-element.23, f32[1024]{0:T(1024)S(1)} %get-tuple-element.24), channel_id=1, replica_groups=mesh['dp_0'=4,'dp_1'=2,'tensor_0'=4,'tensor_1'=4] {'tensor_0'}, use_global_device_ids=true, to_apply=%region_3.4 | all-reduce | flops 2048 | bytes 16384 | tf_op jit(solution)/shard_map/psum | solution.py:35
  180.3 10.1 %all-reduce.1 = (f32[1024]{0:T(1024)S(1)}, f32[1024]{0:T(1024)S(1)}) all-reduce(f32[1024]{0:T(1024)S(1)} %get-tuple-element.13, f32[1024]{0:T(1024)S(1)} %get-tuple-element.14), channel_id=1, replica_groups=mesh['dp_0'=4,'dp_1'=2,'tensor_0'=4,'tensor_1'=4] {'tensor_1'}, use_global_device_ids=true, to_apply=%region_4.5 | all-reduce | flops 2048 | bytes 16384 | tf_op jit(solution)/shard_map/psum | solution.py:35
  190.4 0.8 fusion.35
  191.2 0.6 reshape.259
  192.5 8.5 %all-reduce.4 = (f32[]{:T(128)}, f32[]{:T(128)}, f32[]{:T(128)}) all-reduce(f32[]{:T(128)S(6)} %neg.3, f32[]{:T(128)} %get-tuple-element.4, f32[]{:T(128)} %get-tuple-element.3), channel_id=1, replica_groups=mesh['dp_0'=4,'dp_1'=2,'tensor_0'=4,'tensor_1'=4] {'dp_0'}, use_global_device_ids=true, to_apply=%region_11.12 | all-reduce | flops 3 | bytes 24 | tf_op jit(solution)/shard_map/psum | solution.py:35
  201.0 3.1 %all-reduce.6 = (f32[]{:T(128)}, f32[]{:T(128)}, f32[]{:T(128)}) all-reduce(f32[]{:T(128)} %get-tuple-element.15, f32[]{:T(128)} %get-tuple-element.16, f32[]{:T(128)} %get-tuple-element.17), channel_id=1, replica_groups=mesh['dp_0'=4,'dp_1'=2,'tensor_0'=4,'tensor_1'=4] {'dp_1'}, use_global_device_ids=true, to_apply=%region_12.13 | all-reduce | flops 3 | bytes 24 | tf_op jit(solution)/shard_map/psum | solution.py:35
  204.1 10.3 %all-reduce.2 = (f32[]{:T(128)}, f32[]{:T(128)}, f32[]{:T(128)}) all-reduce(f32[]{:T(128)} %get-tuple-element.20, f32[]{:T(128)} %get-tuple-element.21, f32[]{:T(128)} %get-tuple-element.22), channel_id=1, replica_groups=mesh['dp_0'=4,'dp_1'=2,'tensor_0'=4,'tensor_1'=4] {'tensor_0'}, use_global_device_ids=true, to_apply=%region_13.14 | all-reduce | flops 3 | bytes 24 | tf_op jit(solution)/shard_map/psum | solution.py:35
  214.4 9.7 %all-reduce = (f32[]{:T(128)}, f32[]{:T(128)}, f32[]{:T(128)}) all-reduce(f32[]{:T(128)} %get-tuple-element.10, f32[]{:T(128)} %get-tuple-element.11, f32[]{:T(128)} %get-tuple-element.12), channel_id=1, replica_groups=mesh['dp_0'=4,'dp_1'=2,'tensor_0'=4,'tensor_1'=4] {'tensor_1'}, use_global_device_ids=true, to_apply=%region_14.15 | all-reduce | flops 3 | bytes 24 | tf_op jit(solution)/shard_map/psum | solution.py:35
  (11 shorter events, 0.1 us)
Async XLA Ops:
  7.2 82.6 %copy-start.1 = (f32[4608]{0:T(1024)S(1)}, f32[4608]{0:T(1024)}, u32[]{:S(2)}) copy-start(f32[4608]{0:T(1024)} %param.6) | copy-start | bytes 55300
  7.2 76.8 %all-gather.6.cloned.1.call-start = ((), (), s32[]{:S(2)}) async-start(), calls=%async_computation | async-start | bytes 9510912 | tf_op jit(solution)/shard_map/all_gather | solution.py:60
  84.0 6.4 %copy-start = (bf16[1024,4608]{1,0:T(8,128)(2,1)S(1)}, bf16[1024,4608]{1,0:T(8,128)(2,1)}, u32[]{:S(2)}) copy-start(bf16[1024,4608]{1,0:T(8,128)(2,1)} %all-gather.6.cloned.1.call-done) | copy-start | bytes 28311556
Sparse Core Ops, SparseCore 0:
  11.1 72.8 all-gather.5
where the time goes:
time: 237 us; the launch traced here: 236 us
  blocking collectives  96.5 us (41%)
  local copies, waits for them, and re-layouts  51.3 us (22%)
  matrix products  26.1 us (11%)
  waiting for transfers between devices  24.7 us (10%)
  between operations  19.7 us (8%)
  other arithmetic  17.3 us (7%)
    psum x8, blocking collectives, one_axis_at_a_time(): value = lax.psum(value, axis)  60.4 us
    gather x1, local copies, waits for them, and re-layouts, per_device(): jnp.take_along_axis(capped, jnp.clip(local, 0, vocab_dev - 1)[:, None], a...  45.1 us
    all_gather x4, blocking collectives, gather_in_order(): pieces = lax.all_gather(pieces, axes[k], axis=0, tiled=True)  36.2 us
    dot_general x1, matrix products, per_device(): lax.dot_general(rows, embed, (((1,), (1,)), ((), ())), preferred_element_...  26.1 us
    all_gather x1, waiting for transfers between devices, per_device(): rows = normalize(lax.all_gather(flat, DP_TENSOR, axis=0, tiled=True), gain)  24.7 us
    convert_element_type x1, other arithmetic, per_device(): live_all = (positions < jnp.take(lengths, batch_ids)).astype(jnp.float32)  5.82 us
    reduce_sum x1, other arithmetic, normalize(): meansq = jnp.mean(values * values, axis=-1, keepdims=True)  5.72 us
    gather x10, other arithmetic, per_device(): live_all = (positions < jnp.take(lengths, batch_ids)).astype(jnp.float32)  4.91 us
  transfers between devices with their start and end apart: 1, of which 1 were waited for; matrix products, arithmetic and copies ran while one was open for 6% of the time, Pallas kernels for 0%

commit v1 on v0

--- a/solution.py
+++ b/solution.py
@@ -8,6 +8,11 @@
 TENSOR = ("tensor_0", "tensor_1")
 DP = ("dp_0", "dp_1")
 DP_TENSOR = ("dp_0", "dp_1", "tensor_0", "tensor_1")
+
+
+def all_by_exchange(x, axis, dim):
+    outgoing = jnp.stack([x] * lax.axis_size(axis))
+    return jnp.concatenate(lax.all_to_all(outgoing, axis, 0, 0), axis=dim)
 
 
 def joined_along(pieces, dim):
@@ -57,7 +62,7 @@
     positions = owner % n_tensor * stretch + within % stretch
     live_all = (positions < jnp.take(lengths, batch_ids)).astype(jnp.float32)
     all_labels = gathered_by_axis(labels.reshape(rows_local), DP_TENSOR, (0, 2, 3, 1), 0)
-    rows = normalize(lax.all_gather(flat, DP_TENSOR, axis=0, tiled=True), gain)
+    rows = normalize(all_by_exchange(flat, DP_TENSOR, 0), gain)
     values = lax.dot_general(
         rows, embed, (((1,), (1,)), ((), ())), preferred_element_type=jnp.float32
     )

time: 237 us -> 325 us (1.37)
  blocking collectives: 96.5 us -> 208 us
  waiting for transfers between devices: 24.7 us -> 0.01 us
  between operations: 19.7 us -> 6.33 us
  starting transfers between devices: 0.04 us -> 11.6 us
    all_gather x4, blocking collectives: 36.2 us -> 148 us  [gather_in_order(): pieces = lax.all_gather(pieces, axes[k], axis=0, tiled=True)]
    all_gather x1 -> x0, waiting for transfers between devices: 24.7 us -> none  [per_device(): rows = normalize(lax.all_gather(flat, DP_TENSOR, axis=0, tiled=True), gain)]
    all_to_all x0 -> x1, starting transfers between devices: none -> 11.6 us  [all_by_exchange(): return jnp.concatenate(lax.all_to_all(outgoing, axis, 0, 0), axis=dim)]
    another operation x0 -> x2, local copies, waits for them, and re-layouts: none -> 5.17 us  [all_by_exchange(): outgoing = jnp.stack([x] * lax.axis_size(axis))]
  transfers between devices with their start and end apart: 1 -> 1, of which waited for: 1 -> 0; matrix products, arithmetic and copies ran while one was open for 6% -> 4% of each run, Pallas kernels for 0% -> 0%
where the time goes in v1:
time: 325 us; the launch traced here: 323 us
  blocking collectives  208 us (64%)
  local copies, waits for them, and re-layouts  52.5 us (16%)
  matrix products  27.9 us (9%)
  other arithmetic  17 us (5%)
  starting transfers between devices  11.6 us (4%)
  between operations  6.33 us (2%)
    all_gather x4, blocking collectives, gather_in_order(): pieces = lax.all_gather(pieces, axes[k], axis=0, tiled=True)  148 us
    psum x8, blocking collectives, one_axis_at_a_time(): value = lax.psum(value, axis)  60.4 us
    gather x1, local copies, waits for them, and re-layouts, per_device(): jnp.take_along_axis(capped, jnp.clip(local, 0, vocab_dev - 1)[:, None], a...  45 us
    dot_general x1, matrix products, per_device(): lax.dot_general(rows, embed, (((1,), (1,)), ((), ())), preferred_element_...  27.9 us
    all_to_all x1, starting transfers between devices, all_by_exchange(): return jnp.concatenate(lax.all_to_all(outgoing, axis, 0, 0), axis=dim)  11.6 us
  transfers between devices with their start and end apart: 1, of which 0 were waited for; matrix products, arithmetic and copies ran while one was open for 4% of the time, Pallas kernels for 0%

profile of v1, /device:TPU:0, one launch (start us, length us, event | category | flops | bytes accessed | tf_op | source)
XLA Modules:
  0.0 323.5 jit_solution(18150967233153980444)
XLA Ops:
  0.6 0.9 stack_reshape.2
  1.5 4.3 %stack.3 = bf16[128,8,4608]{2,1,0:T(8,128)(2,1)} broadcast(bf16[8,4608]{1,0:T(8,128)(2,1)S(1)} %stack_reshape.2), dimensions={1,2} | broadcast | bytes 9510912 | tf_op jit(solution)/shard_map/stack | solution.py:14
  5.8 0.0 copy-start.2
  5.8 0.0 copy-start
  5.8 11.6 %all-to-all-start = ((bf16[128,8,4608]{2,1,0:T(8,128)(2,1)}), bf16[128,8,4608]{2,1,0:T(8,128)(2,1)}, u32[]{:S(2)}, u32[]{:S(2)}) async-start(bf16[128,8,4608]{2,1,0:T(8,128)(2,1)} %stack.3), calls=%async_computation | async-start | bytes 18874368 | tf_op jit(solution)/shard_map/all_to_all | solution.py:15
  17.5 0.0 copy-done.2
  17.5 0.0 copy-start.1
  17.5 0.1 reshape.341
  17.6 115.6 %all-gather = s32[4,1,8]{2,1,0:T(1,128)S(1)} all-gather(s32[1,1,8]{2,1,0:T(1,128)S(1)} %reshape.341), channel_id=1, replica_groups=mesh['dp_0'=4,'dp_1'=2,'tensor_0'=4,'tensor_1'=4] {'dp_0'}, dimensions={0}, use_global_device_ids=true | all-gather | bytes 160 | tf_op jit(solution)/shard_map/all_gather | solution.py:27
  133.2 17.9 %all-gather.1 = s32[4,4,8]{2,1,0:T(4,128)S(1)} all-gather(s32[1,4,8]{2,1,0:T(4,128)S(1)} %bitcast.49), channel_id=1, replica_groups=mesh['dp_0'=4,'dp_1'=2,'tensor_0'=4,'tensor_1'=4] {'tensor_0'}, dimensions={0}, use_global_device_ids=true | all-gather | bytes 640 | tf_op jit(solution)/shard_map/all_gather | solution.py:27
  151.1 0.1 copy.28
  151.2 12.4 %all-gather.2 = s32[4,16,8]{1,2,0:T(8,128)S(1)} all-gather(s32[1,16,8]{1,2,0:T(8,128)S(1)} %copy.28), channel_id=1, replica_groups=mesh['dp_0'=4,'dp_1'=2,'tensor_0'=4,'tensor_1'=4] {'tensor_1'}, dimensions={0}, use_global_device_ids=true | all-gather | bytes 2560 | tf_op jit(solution)/shard_map/all_gather | solution.py:27
  163.6 0.1 reshape.347
  163.7 1.8 all-gather.3
  165.5 0.1 copy.32
  165.6 0.1 min.24
  165.8 0.1 min.22
  165.9 0.1 copy.30
  166.0 0.1 and.146
  166.1 0.1 compare_reduce_fusion
  166.2 0.1 compare_reduce_fusion.1
  166.3 0.1 compare_reduce_fusion.2
  166.3 0.1 compare_reduce_fusion.3
  166.4 0.1 compare_reduce_fusion.4
  166.4 0.1 compare_reduce_fusion.5
  166.5 0.1 compare_reduce_fusion.6
  166.5 0.1 compare_reduce_fusion.7
  166.6 0.1 compare_reduce_fusion.8
  166.7 0.0 copy-done
  166.7 0.7 fusion.38
  167.3 4.5 %compare_select_fusion.2 = s32[1024,1]{0,1:T(1,128)S(1)} fusion(s32[]{:T(128)} %bitcast.9, s32[]{:T(128)} %bitcast.10, s32[]{:T(128)} %bitcast.11, s32[]{:T(128)} %bitcast.12, s32[]{:T(128)} %bitcast.13, s32[]{:T(128)} %bitcast.15, s32[]{:T(128)} %bitcast.14), kind=kLoop, calls=%fused_computation.24 | loop fusion | flops 60416 | bytes 4124 | tf_op jit(solution)/shard_map/jit(_take)/gather | solution.py:63
  171.9 5.5 %fusion.35 = f32[1024]{0:T(1024)S(1)} fusion(pred[1024]{0:T(1024)(128)(4,1)S(1)} %compare_reduce_fusion, pred[1024]{0:T(1024)(128)(4,1)S(1)} %compare_reduce_fusion.1, pred[1024]{0:T(1024)(128)(4,1)S(1)} %compare_reduce_fusion.2, pred[1024]{0:T(1024)(128)(4,1)S(1)} %compare_reduce_fusion.3, pred[1024]{0:T(1024)(128)(4,1)S(1)} %compare_reduce_fusion.4, ...), kind=kLoop, calls=%fused_computation.91 | loop fusion | flops 73728 | bytes 17444 | tf_op jit(solution)/shard_map/convert_element_type | solution.py:63
  177.5 0.0 all-to-all-done
  177.5 5.6 %fusion.3 = f32[128,8]{1,0:T(8,128)S(1)} fusion(bf16[128,8,4608]{2,1,0:T(8,128)(2,1)} %all-to-all-done), kind=kLoop, calls=%fused_computation.6 | loop fusion | flops 14154752 | bytes 9441280 | tf_op jit(solution)/shard_map/reduce_sum | solution.py:46
  183.1 0.1 rsqrt.12
  183.2 0.0 copy-done.1
  183.2 27.9 %exponential_reduce_fusion = (f32[1024]{0:T(1024)S(1)}, f32[1024,2000]{0,1:T(8,128)}) fusion(bf16[2000,4608]{1,0:T(8,128)(2,1)} %param.9, bf16[128,8,4608]{2,1,0:T(8,128)(2,1)} %all-to-all-done, f32[4608]{0:T(1024)S(1)} %copy-done.1, f32[1024]{0:T(1024)S(1)} %rsqrt.12), kind=kOutput, calls=%fused_computation.10 | convolution fusion | flops 18899386368 | bytes 36087808 | tf_op jit(solution)/shard_map/dot_general | solution.py:66
  211.1 45.0 %gather_fusion = f32[1024]{0:T(1024)S(1)} fusion(f32[1024,2000]{0,1:T(8,128)} %get-tuple-element.46, s32[1024]{0:T(1024)S(1)} %bitcast.44), kind=kCustom, calls=%fused_computation | custom fusion | bytes 16384 | tf_op jit(solution)/shard_map/jit(take_along_axis)/gather | solution.py:74
  256.2 7.8 %all-reduce.5 = (f32[1024]{0:T(1024)S(1)}, f32[1024]{0:T(1024)S(1)}) all-reduce(f32[1024]{0:T(1024)S(1)} %select_select_fusion.1, f32[1024]{0:T(1024)S(1)} %get-tuple-element.45), channel_id=1, replica_groups=mesh['dp_0'=4,'dp_1'=2,'tensor_0'=4,'tensor_1'=4] {'dp_0'}, use_global_device_ids=true, to_apply=%region_1.2 | all-reduce | flops 2048 | bytes 16384 | tf_op jit(solution)/shard_map/psum | solution.py:40
  264.0 2.5 all-reduce.7
  266.5 7.9 %all-reduce.3 = (f32[1024]{0:T(1024)S(1)}, f32[1024]{0:T(1024)S(1)}) all-reduce(f32[1024]{0:T(1024)S(1)} %get-tuple-element.23, f32[1024]{0:T(1024)S(1)} %get-tuple-element.24), channel_id=1, replica_groups=mesh['dp_0'=4,'dp_1'=2,'tensor_0'=4,'tensor_1'=4] {'tensor_0'}, use_global_device_ids=true, to_apply=%region_3.4 | all-reduce | flops 2048 | bytes 16384 | tf_op jit(solution)/shard_map/psum | solution.py:40
  274.4 10.2 %all-reduce.1 = (f32[1024]{0:T(1024)S(1)}, f32[1024]{0:T(1024)S(1)}) all-reduce(f32[1024]{0:T(1024)S(1)} %get-tuple-element.13, f32[1024]{0:T(1024)S(1)} %get-tuple-element.14), channel_id=1, replica_groups=mesh['dp_0'=4,'dp_1'=2,'tensor_0'=4,'tensor_1'=4] {'tensor_1'}, use_global_device_ids=true, to_apply=%region_4.5 | all-reduce | flops 2048 | bytes 16384 | tf_op jit(solution)/shard_map/psum | solution.py:40
  284.6 0.8 fusion.36
  285.4 0.6 reshape.269
  286.7 10.5 %all-reduce.4 = (f32[]{:T(128)}, f32[]{:T(128)}, f32[]{:T(128)}) all-reduce(f32[]{:T(128)S(6)} %neg.3, f32[]{:T(128)} %get-tuple-element.4, f32[]{:T(128)} %get-tuple-element.3), channel_id=1, replica_groups=mesh['dp_0'=4,'dp_1'=2,'tensor_0'=4,'tensor_1'=4] {'dp_0'}, use_global_device_ids=true, to_apply=%region_11.12 | all-reduce | flops 3 | bytes 24 | tf_op jit(solution)/shard_map/psum | solution.py:40
  297.2 3.1 all-reduce.6
  300.3 9.7 %all-reduce.2 = (f32[]{:T(128)}, f32[]{:T(128)}, f32[]{:T(128)}) all-reduce(f32[]{:T(128)} %get-tuple-element.20, f32[]{:T(128)} %get-tuple-element.21, f32[]{:T(128)} %get-tuple-element.22), channel_id=1, replica_groups=mesh['dp_0'=4,'dp_1'=2,'tensor_0'=4,'tensor_1'=4] {'tensor_0'}, use_global_device_ids=true, to_apply=%region_13.14 | all-reduce | flops 3 | bytes 24 | tf_op jit(solution)/shard_map/psum | solution.py:40
  310.0 8.7 %all-reduce = (f32[]{:T(128)}, f32[]{:T(128)}, f32[]{:T(128)}) all-reduce(f32[]{:T(128)} %get-tuple-element.10, f32[]{:T(128)} %get-tuple-element.11, f32[]{:T(128)} %get-tuple-element.12), channel_id=1, replica_groups=mesh['dp_0'=4,'dp_1'=2,'tensor_0'=4,'tensor_1'=4] {'tensor_1'}, use_global_device_ids=true, to_apply=%region_14.15 | all-reduce | flops 3 | bytes 24 | tf_op jit(solution)/shard_map/psum | solution.py:40
  (11 shorter events, 0.1 us)
Async XLA Ops:
  5.8 11.7 %copy-start.2 = (s32[2,4]{1,0:T(2,128)S(1)}, s32[2,4]{1,0:T(2,128)}, u32[]{:S(2)}) copy-start(s32[2,4]{1,0:T(2,128)} %param.7) | copy-start | bytes 100
  5.8 160.9 %copy-start = (s32[16]{0:T(128)S(1)}, s32[16]{0:T(128)}, u32[]{:S(2)}) copy-start(s32[16]{0:T(128)} %param.8) | copy-start | bytes 196
  5.8 171.7 %all-to-all-start = ((bf16[128,8,4608]{2,1,0:T(8,128)(2,1)}), bf16[128,8,4608]{2,1,0:T(8,128)(2,1)}, u32[]{:S(2)}, u32[]{:S(2)}) async-start(bf16[128,8,4608]{2,1,0:T(8,128)(2,1)} %stack.3), calls=%async_computation | async-start | bytes 18874368 | tf_op jit(solution)/shard_map/all_to_all | solution.py:15
  17.5 165.7 %copy-start.1 = (f32[4608]{0:T(1024)S(1)}, f32[4608]{0:T(1024)}, u32[]{:S(2)}) copy-start(f32[4608]{0:T(1024)} %param.6) | copy-start | bytes 55300
